TPU v7x, 32 devices: a whole 2x2x4 slice. The times are simulated.
32 devices in a mesh: dp: 4 (over y, core), tensor: 2 (over x), pipe: 4 (over z).
Axes of the slice: x: 2, y: 2, z: 4, core: 2. Of those that a mesh axis runs over, the one named last changes fastest.
Arguments:
- grad_parts: float32 [4, 4, 2, 64, 8192], P('dp', 'pipe', 'tensor'), may hold values from -24 to 24
- drop_flags: int32 [4, 4, 2, 64], P('dp', 'pipe', 'tensor'), may hold values from 0 to 1, as said below
- owner_order: int32 [4], replicated, may hold values from 0 to 3, each once
- step_count: int32 [], replicated, may hold values from 1 to 11
- master: float32 [4, 2, 64, 8192], P('pipe', 'tensor', None, 'dp'), may hold values from -6 to 6
- moment_m: float32 [4, 2, 64, 8192], P('pipe', 'tensor', None, 'dp'), may hold values from -0.15625 to 0.15625
- moment_v: float32 [4, 2, 64, 8192], P('pipe', 'tensor', None, 'dp'), may hold values from 0.0001 to 0.001
Outputs:
- new_master: float32 [4, 2, 64, 8192], P('pipe', 'tensor', None, 'dp')
- new_m: float32 [4, 2, 64, 8192], P('pipe', 'tensor', None, 'dp')
- new_v: float32 [4, 2, 64, 8192], P('pipe', 'tensor', None, 'dp')
- direction: float32 [4, 2, 64, 8192], P('pipe', 'tensor', None, 'dp')
- dropped_total: int32 [], replicated
Inputs may be any that keep to these rules, and one draw needn't show every extreme that they name: `drop_flags`: A row may be flagged by every replica.
All inputs are finite; a program needn't handle non-finite values.
Results may differ from a plain program's by a relative error of at most 0.0003.
Values sent between devices are 32-bit elements; how exact they have to be, the bound alone decides.
No kernel may reach another device: no remote copies, remote signals or barrier semaphores. Data moves between devices by JAX's collectives and lax.ppermute only.
A program may use at most 64 MiB of HBM per device.

v0:
```python
import jax
import jax.numpy as jnp
from jax import lax
from jax.sharding import PartitionSpec as P


def body(grad_parts, drop_flags, owner_order, step_count, master, moment_m, moment_v):
    replicas = lax.axis_size("dp")
    flags = drop_flags[0, 0, 0]
    kept = (1 - flags).astype(jnp.float32)
    local_grad = grad_parts[0, 0, 0]
    rows_here = local_grad.shape[0]
    width = local_grad.shape[1]
    block_cols = width // replicas
    term = local_grad * kept[:, None]
    blocks = jnp.take(term.reshape(rows_here, replicas, block_cols), owner_order, axis=1)
    received = lax.all_to_all(blocks, "dp", split_axis=1, concat_axis=1, tiled=True)
    summed = jnp.sum(received, axis=1)
    count = lax.psum(kept, "dp")
    grad = summed / jnp.maximum(count, 1.0)[:, None]
    square_sum, dropped = lax.psum(
        (jnp.sum(grad * grad), jnp.sum(flags).astype(jnp.float32)), ("dp", "tensor", "pipe")
    )
    entries = rows_here * width * lax.axis_size("tensor") * lax.axis_size("pipe")
    rms = jnp.sqrt(square_sum / entries)
    clip = jnp.minimum(1.0, 0.05 / (rms + 1e-06))
    scaled = clip * grad
    old_m = moment_m[0, 0]
    old_v = moment_v[0, 0]
    weights = master[0, 0]
    new_m = 0.9 * old_m + 0.1 * scaled
    new_v = 0.999 * old_v + 0.001 * scaled * scaled
    steps = step_count.astype(jnp.float32)
    m_hat = new_m / (1.0 - jnp.power(0.9, steps))
    v_hat = new_v / (1.0 - jnp.power(0.999, steps))
    direction = m_hat / (jnp.sqrt(v_hat) + 1e-08) + 0.1 * weights
    new_master = weights - 0.001 * direction
    return (
        new_master[None, None],
        new_m[None, None],
        new_v[None, None],
        direction[None, None],
        dropped.astype(jnp.int32),
    )


def solution(mesh):
    return jax.shard_map(
        body,
        mesh=mesh,
        in_specs=(
            P("dp", "pipe", "tensor", None, None),
            P("dp", "pipe", "tensor", None),
            P(),
            P(),
            P("pipe", "tensor", None, "dp"),
            P("pipe", "tensor", None, "dp"),
            P("pipe", "tensor", None, "dp"),
        ),
        out_specs=(
            P("pipe", "tensor", None, "dp"),
            P("pipe", "tensor", None, "dp"),
            P("pipe", "tensor", None, "dp"),
            P("pipe", "tensor", None, "dp"),
            P(),
        ),
        check_vma=False,
    )
```

profile of v0, /device:TPU:0, one launch (start us, length us, event | category | flops | bytes accessed | tf_op | source)
XLA Modules:
  0.0 91.8 jit_solution(3209272403787313384)
XLA Ops:
  0.6 0.7 compare_select_fusion
  1.3 0.7 compare_and_fusion
  2.0 1.3 %fusion.3 = (s32[]{:T(128)}, f32[64]{0:T(128)S(1)}) fusion(s32[1,1,1,64]{3,2,1,0:T(1,128)} %param.8), kind=kLoop, calls=%fused_computation.16 | loop fusion | flops 191 | bytes 516 | tf_op jit(solution)/shard_map/reduce_sum | solution.py:22
  3.2 2.7 %squeeze.2 = f32[64,4,2048]{2,1,0:T(4,128)S(1)} reshape(f32[1,1,1,64,8192]{4,3,2,1,0:T(8,128)} %param.7) | data formatting | bytes 4194304 | tf_op jit(solution)/shard_map/squeeze | solution.py:11
  5.9 2.6 %copy_multiply_fusion = f32[64,4,2048]{2,0,1:T(8,128)} fusion(f32[64,4,2048]{2,1,0:T(4,128)S(1)} %squeeze.2, f32[64]{0:T(128)S(1)} %get-tuple-element.12), kind=kLoop, calls=%fused_computation.1 | loop fusion | flops 524288 | bytes 4194560 | tf_op jit(solution)/shard_map/mul | solution.py:15
  8.5 2.3 %gather_fusion = f32[4,64,2048]{2,1,0:T(8,128)S(1)} fusion(f32[64,4,2048]{2,0,1:T(8,128)} %copy_multiply_fusion, s32[1024]{0:T(1024)S(1)} %pad_clamp_fusion), kind=kCustom, calls=%fused_computation | custom fusion | bytes 4194320 | tf_op jit(solution)/shard_map/jit(_take)/gather | solution.py:16
  10.8 1.6 %select_bitcast_fusion = f32[64,4,2048]{2,0,1:T(8,128)} fusion(f32[4,64,2048]{2,1,0:T(8,128)S(1)} %gather_fusion, pred[4]{0:T(512)(128)(4,1)S(1)} %compare_and_fusion), kind=kLoop, calls=%fused_computation.2 | loop fusion | flops 524288 | bytes 4194308 | tf_op jit(solution)/shard_map/jit(_take)/select_n | solution.py:16
  12.4 4.3 %all-to-all-start = ((f32[64,4,2048]{2,0,1:T(8,128)}), f32[64,4,2048]{2,0,1:T(8,128)S(1)}, u32[]{:S(2)}, u32[]{:S(2)}) async-start(f32[64,4,2048]{2,0,1:T(8,128)} %select_bitcast_fusion), calls=%async_computation | async-start | bytes 4194304 | tf_op jit(solution)/shard_map/all_to_all | solution.py:17
  16.7 0.0 copy-start
  18.1 25.7 %psum.21 = f32[64]{0:T(128)S(1)} all-reduce(f32[64]{0:T(128)S(1)} %get-tuple-element.12), channel_id=1, replica_groups=mesh['dp'=4,'tensor'=2,'pipe'=4] {'dp'}, use_global_device_ids=true, to_apply=%region_1.2 | all-reduce | flops 64 | bytes 512 | tf_op jit(solution)/shard_map/psum | solution.py:19
  43.8 0.0 all-to-all-done
  43.8 0.2 reduce_sum.29
  44.0 0.8 multiply_reduce_fusion
  44.8 41.6 %all-reduce = (f32[]{:T(128)}, f32[]{:T(128)}) all-reduce(f32[]{:T(128)} %multiply_reduce_fusion, f32[]{:T(128)S(6)} %convert_element_type.22), channel_id=1, replica_groups=mesh['dp'=4,'tensor'=2,'pipe'=4] {'dp','tensor','pipe'}, use_global_device_ids=true, to_apply=%region_3.4 | all-reduce | flops 2 | bytes 16 | tf_op jit(solution)/shard_map/psum | solution.py:21
  87.8 0.0 copy-done
  87.8 2.9 %multiply_subtract_fusion = (f32[1,1,64,2048]{3,2,1,0:T(8,128)}, f32[1,1,64,2048]{3,2,1,0:T(8,128)}, f32[1,1,64,2048]{3,2,1,0:T(8,128)}, f32[1,1,64,2048]{3,2,1,0:T(8,128)}) fusion(f32[1,1,64,2048]{3,2,1,0:T(8,128)S(1)} %copy-done, f32[]{:T(128)S(6)} %sub.24, f32[]{:T(128)S(6)} %sub.23, f32[64]{0:T(128)S(1)} %broadcast_maximum_fusion, ...), kind=kLoop, calls=%fused_computation.7 | loop fusion | flops 2228224 | bytes 4194572 | tf_op jit(solution)/shard_map/sub | solution.py:37
  (2 shorter events, 0.0 us)
Async XLA Ops:
  12.4 31.4 %all-to-all-start = ((f32[64,4,2048]{2,0,1:T(8,128)}), f32[64,4,2048]{2,0,1:T(8,128)S(1)}, u32[]{:S(2)}, u32[]{:S(2)}) async-start(f32[64,4,2048]{2,0,1:T(8,128)} %select_bitcast_fusion), calls=%async_computation | async-start | bytes 4194304 | tf_op jit(solution)/shard_map/all_to_all | solution.py:17
  16.7 71.1 %copy-start = (f32[1,1,64,2048]{3,2,1,0:T(8,128)S(1)}, f32[1,1,64,2048]{3,2,1,0:T(8,128)}, u32[]{:S(2)}) copy-start(f32[1,1,64,2048]{3,2,1,0:T(8,128)} %param.11) | copy-start | bytes 1572868
where the time goes:
time: 92.3 us; the launch traced here: 91.8 us
  blocking collectives  67.3 us (73%)
  other arithmetic  10.7 us (12%)
  local copies, waits for them, and re-layouts  4.94 us (5%)
  between operations  4.63 us (5%)
  starting transfers between devices  4.26 us (5%)
    psum x1, blocking collectives, body(): lax.psum((jnp.sum(grad * grad), jnp.sum(flags).astype(jnp.float32)), ('dp...  41.6 us
    psum x1, blocking collectives, body(): count = lax.psum(kept, 'dp')  25.7 us
    all_to_all x1, starting transfers between devices, body(): lax.all_to_all(blocks, 'dp', split_axis=1, concat_axis=1, tiled=True)  4.26 us
    sub x1, other arithmetic, body(): new_master = weights - 0.001 * direction  2.86 us
    squeeze x1, local copies, waits for them, and re-layouts, body(): local_grad = grad_parts[0, 0, 0]  2.67 us
    mul x1, other arithmetic, body(): term = local_grad * kept[:, None]  2.57 us
    select_n x2, other arithmetic, body(): jnp.take(term.reshape(rows_here, replicas, block_cols), owner_order, axis=1)  2.3 us
    gather x1, local copies, waits for them, and re-layouts, body(): jnp.take(term.reshape(rows_here, replicas, block_cols), owner_order, axis=1)  2.27 us
  transfers between devices with their start and end apart: 1, of which 0 were waited for; matrix products, arithmetic and copies ran while one was open for 0% of the time, Pallas kernels for 0%

commit v1 on v0

--- a/solution.py
+++ b/solution.py
@@ -2,6 +2,10 @@
 import jax.numpy as jnp
 from jax import lax
 from jax.sharding import PartitionSpec as P
+
+
+def advance_shards(x_part, a_name):
+    return jnp.sum(lax.all_gather(x_part, a_name), axis=0)
 
 
 def body(grad_parts, drop_flags, owner_order, step_count, master, moment_m, moment_v):
@@ -16,7 +20,7 @@
     blocks = jnp.take(term.reshape(rows_here, replicas, block_cols), owner_order, axis=1)
     received = lax.all_to_all(blocks, "dp", split_axis=1, concat_axis=1, tiled=True)
     summed = jnp.sum(received, axis=1)
-    count = lax.psum(kept, "dp")
+    count = advance_shards(kept, "dp")
     grad = summed / jnp.maximum(count, 1.0)[:, None]
     square_sum, dropped = lax.psum(
         (jnp.sum(grad * grad), jnp.sum(flags).astype(jnp.float32)), ("dp", "tensor", "pipe")

time: 92.3 us -> 90.6 us (0.982)
  blocking collectives: 67.3 us -> 65.6 us
    psum x1 -> x0, blocking collectives: 25.7 us -> none  [body(): count = lax.psum(kept, 'dp')]
    all_gather x0 -> x1, blocking collectives: none -> 25.1 us  [advance_shards(): return jnp.sum(lax.all_gather(x_part, a_name), axis=0)]
    psum x1, blocking collectives: 41.6 us -> 40.5 us  [body(): lax.psum((jnp.sum(grad * grad), jnp.sum(flags).astype(jnp.float32)), ('dp...]
where the time goes in v1:
time: 90.6 us; the launch traced here: 90.2 us
  blocking collectives  65.6 us (72%)
  other arithmetic  10.7 us (12%)
  local copies, waits for them, and re-layouts  4.94 us (5%)
  between operations  4.64 us (5%)
  starting transfers between devices  4.26 us (5%)
    psum x1, blocking collectives, body(): lax.psum((jnp.sum(grad * grad), jnp.sum(flags).astype(jnp.float32)), ('dp...  40.5 us
    all_gather x1, blocking collectives, advance_shards(): return jnp.sum(lax.all_gather(x_part, a_name), axis=0)  25.1 us
    all_to_all x1, starting transfers between devices, body(): lax.all_to_all(blocks, 'dp', split_axis=1, concat_axis=1, tiled=True)  4.26 us
    sub x1, other arithmetic, body(): new_master = weights - 0.001 * direction  2.86 us
    squeeze x1, local copies, waits for them, and re-layouts, body(): local_grad = grad_parts[0, 0, 0]  2.67 us
    mul x1, other arithmetic, body(): term = local_grad * kept[:, None]  2.57 us
    select_n x2, other arithmetic, body(): jnp.take(term.reshape(rows_here, replicas, block_cols), owner_order, axis=1)  2.3 us
    gather x1, local copies, waits for them, and re-layouts, body(): jnp.take(term.reshape(rows_here, replicas, block_cols), owner_order, axis=1)  2.27 us
  transfers between devices with their start and end apart: 1, of which 0 were waited for; matrix products, arithmetic and copies ran while one was open for 0% of the time, Pallas kernels for 0%

profile of v1, /device:TPU:0, one launch (start us, length us, event | category | flops | bytes accessed | tf_op | source)
XLA Modules:
  0.0 90.2 jit_solution(14291898204369937056)
XLA Ops:
  0.6 0.7 compare_select_fusion
  1.3 0.7 compare_and_fusion
  2.0 1.3 %fusion.4 = (s32[]{:T(128)}, f32[64]{0:T(128)S(1)}, f32[1,1,1,64]{3,2,1,0:T(1,128)S(1)}) fusion(s32[1,1,1,64]{3,2,1,0:T(1,128)} %param.8), kind=kLoop, calls=%fused_computation.17 | loop fusion | flops 191 | bytes 772 | tf_op jit(solution)/shard_map/reduce_sum | solution.py:26
  3.2 2.7 %squeeze.2 = f32[64,4,2048]{2,1,0:T(4,128)S(1)} reshape(f32[1,1,1,64,8192]{4,3,2,1,0:T(8,128)} %param.7) | data formatting | bytes 4194304 | tf_op jit(solution)/shard_map/squeeze | solution.py:15
  5.9 2.6 %copy_multiply_fusion = f32[64,4,2048]{2,0,1:T(8,128)} fusion(f32[64,4,2048]{2,1,0:T(4,128)S(1)} %squeeze.2, f32[64]{0:T(128)S(1)} %get-tuple-element.12), kind=kLoop, calls=%fused_computation.1 | loop fusion | flops 524288 | bytes 4194560 | tf_op jit(solution)/shard_map/mul | solution.py:19
  8.5 2.3 %gather_fusion = f32[4,64,2048]{2,1,0:T(8,128)S(1)} fusion(f32[64,4,2048]{2,0,1:T(8,128)} %copy_multiply_fusion, s32[1024]{0:T(1024)S(1)} %pad_clamp_fusion), kind=kCustom, calls=%fused_computation | custom fusion | bytes 4194320 | tf_op jit(solution)/shard_map/jit(_take)/gather | solution.py:20
  10.8 1.6 %select_bitcast_fusion = f32[64,4,2048]{2,0,1:T(8,128)} fusion(f32[4,64,2048]{2,1,0:T(8,128)S(1)} %gather_fusion, pred[4]{0:T(512)(128)(4,1)S(1)} %compare_and_fusion), kind=kLoop, calls=%fused_computation.2 | loop fusion | flops 524288 | bytes 4194308 | tf_op jit(solution)/shard_map/jit(_take)/select_n | solution.py:20
  12.4 4.3 %all-to-all-start = ((f32[64,4,2048]{2,0,1:T(8,128)}), f32[64,4,2048]{2,0,1:T(8,128)S(1)}, u32[]{:S(2)}, u32[]{:S(2)}) async-start(f32[64,4,2048]{2,0,1:T(8,128)} %select_bitcast_fusion), calls=%async_computation | async-start | bytes 4194304 | tf_op jit(solution)/shard_map/all_to_all | solution.py:21
  16.7 0.0 copy-start
  18.1 25.1 %all-gather = f32[4,1,1,64]{3,2,1,0:T(1,128)S(1)} all-gather(f32[1,1,1,64]{3,2,1,0:T(1,128)S(1)} %get-tuple-element.13), channel_id=2, replica_groups=mesh['dp'=4,'tensor'=2,'pipe'=4] {'dp'}, dimensions={0}, use_global_device_ids=true | all-gather | bytes 1280 | tf_op jit(solution)/shard_map/all_gather | solution.py:8
  43.3 0.0 all-to-all-done
  43.3 0.2 reduce_sum.38
  43.5 0.8 multiply_reduce_fusion
  44.3 40.5 %all-reduce = (f32[]{:T(128)}, f32[]{:T(128)}) all-reduce(f32[]{:T(128)} %multiply_reduce_fusion, f32[]{:T(128)S(6)} %convert_element_type.33), channel_id=1, replica_groups=mesh['dp'=4,'tensor'=2,'pipe'=4] {'dp','tensor','pipe'}, use_global_device_ids=true, to_apply=%region_3.4 | all-reduce | flops 2 | bytes 16 | tf_op jit(solution)/shard_map/psum | solution.py:25
  86.2 0.0 copy-done
  86.2 2.9 %multiply_subtract_fusion = (f32[1,1,64,2048]{3,2,1,0:T(8,128)}, f32[1,1,64,2048]{3,2,1,0:T(8,128)}, f32[1,1,64,2048]{3,2,1,0:T(8,128)}, f32[1,1,64,2048]{3,2,1,0:T(8,128)}) fusion(f32[1,1,64,2048]{3,2,1,0:T(8,128)S(1)} %copy-done, f32[]{:T(128)S(6)} %sub.32, f32[]{:T(128)S(6)} %sub.31, f32[64]{0:T(128)S(1)} %broadcast_maximum_fusion, ...), kind=kLoop, calls=%fused_computation.7 | loop fusion | flops 2228224 | bytes 4194572 | tf_op jit(solution)/shard_map/sub | solution.py:41
  (3 shorter events, 0.0 us)
Async XLA Ops:
  12.4 30.9 %all-to-all-start = ((f32[64,4,2048]{2,0,1:T(8,128)}), f32[64,4,2048]{2,0,1:T(8,128)S(1)}, u32[]{:S(2)}, u32[]{:S(2)}) async-start(f32[64,4,2048]{2,0,1:T(8,128)} %select_bitcast_fusion), calls=%async_computation | async-start | bytes 4194304 | tf_op jit(solution)/shard_map/all_to_all | solution.py:21
  16.7 69.5 %copy-start = (f32[1,1,64,2048]{3,2,1,0:T(8,128)S(1)}, f32[1,1,64,2048]{3,2,1,0:T(8,128)}, u32[]{:S(2)}) copy-start(f32[1,1,64,2048]{3,2,1,0:T(8,128)} %param.11) | copy-start | bytes 1572868
